TPU v7x, 32 devices: a whole 2x2x4 slice. The times are simulated.
32 devices in a mesh: blk: 8 (over z, x), dp: 4 (over y, core).
Axes of the slice: x: 2, y: 2, z: 4, core: 2. Of those that a mesh axis runs over, the one named last changes fastest.
Arguments:
- images: bfloat16 [4096, 768], P(('dp', 'blk')), parts along dimension 0, may hold values from -4 to 4
- texts: bfloat16 [4096, 768], P(('dp', 'blk')), parts along dimension 0, may hold values from -4 to 4
- scale: float32 [1], replicated, may hold values from 10 to 20
- cotangent: float32 [2, 4096], P(None, ('dp', 'blk')), parts along dimension 1, may hold values from 0.5 to 2
Outputs:
- row_losses: float32 [2, 4096], P(None, ('dp', 'blk')), parts along dimension 1
- grad_images: float32 [4096, 768], P(('dp', 'blk')), parts along dimension 0
- grad_texts: float32 [4096, 768], P(('dp', 'blk')), parts along dimension 0
There are 4 independent parts, one for each index of `dp`. A program takes and returns all parts, laid end to end along the dimension named above; an argument that names none is the same for every part. Nothing has to cross between parts.
All inputs are finite; a program needn't handle non-finite values.
Results may differ from a plain program's by a relative error of at most 0.0019.
Values may be sent and summed in bfloat16 or wider, within the bound.
A program may use at most 64 MiB of HBM per device.

v0:
```python
import jax
import jax.numpy as jnp
from jax import lax
from jax.sharding import PartitionSpec as P


def dot_rows(left, right):
    return lax.dot_general(
        left, right, (((1,), (1,)), ((), ())), preferred_element_type=jnp.float32
    )


def dot_lead(left, right):
    return lax.dot_general(
        left, right, (((0,), (0,)), ((), ())), preferred_element_type=jnp.float32
    )


def merge_pair(first, second):
    max_new = jnp.maximum(first[0], second[0])
    return (
        max_new,
        first[1] * jnp.exp(first[0] - max_new) + second[1] * jnp.exp(second[0] - max_new),
    )


def block_stats(scores, along):
    top_value = jnp.max(scores, axis=along)
    total_sum = jnp.sum(jnp.exp(scores - jnp.expand_dims(top_value, along)), axis=along)
    return (top_value, total_sum)


def shards(images, texts, scale, cotangent):
    row_count = images.shape[0]
    logit_scale = scale[0]
    cot_rows = cotangent[0]
    cot_cols = cotangent[1]
    low_start = jnp.full((row_count,), -1e30, jnp.float32)
    zero_sums = jnp.zeros((row_count,), jnp.float32)
    all_images, all_texts = (
        lax.all_gather(images, "blk", axis=0, tiled=True),
        lax.all_gather(texts, "blk", axis=0, tiled=True),
    )
    batch_total = all_images.shape[0]
    block_width = min(batch_total, 1024)
    block_count = batch_total // block_width

    def first_pass(step, carried):
        row_part, col_part = carried
        text_block = lax.dynamic_slice_in_dim(all_texts, step * block_width, block_width, 0)
        image_block = lax.dynamic_slice_in_dim(all_images, step * block_width, block_width, 0)
        row_scores = logit_scale * dot_rows(text_block, images)
        col_scores = logit_scale * dot_rows(image_block, texts)
        return (
            merge_pair(row_part, block_stats(row_scores, 0)),
            merge_pair(col_part, block_stats(col_scores, 0)),
        )

    row_part, col_part = lax.fori_loop(
        0, block_count, first_pass, ((low_start, zero_sums), (low_start, zero_sums))
    )
    row_lse = row_part[0] + jnp.log(row_part[1])
    col_lse = col_part[0] + jnp.log(col_part[1])
    matched = logit_scale * jnp.sum(images.astype(jnp.float32) * texts.astype(jnp.float32), axis=1)
    row_losses = jnp.stack([row_lse - matched, col_lse - matched])
    all_row_lse, all_col_lse, all_cot_rows, all_cot_cols = (
        lax.all_gather(row_lse, "blk", axis=0, tiled=True),
        lax.all_gather(col_lse, "blk", axis=0, tiled=True),
        lax.all_gather(cot_rows, "blk", axis=0, tiled=True),
        lax.all_gather(cot_cols, "blk", axis=0, tiled=True),
    )

    def second_pass(step, carried):
        acc_images, acc_texts = carried
        start = step * block_width
        text_block = lax.dynamic_slice_in_dim(all_texts, start, block_width, 0)
        image_block = lax.dynamic_slice_in_dim(all_images, start, block_width, 0)
        col_lse_block = lax.dynamic_slice_in_dim(all_col_lse, start, block_width, 0)
        col_cot_block = lax.dynamic_slice_in_dim(all_cot_cols, start, block_width, 0)
        row_lse_block = lax.dynamic_slice_in_dim(all_row_lse, start, block_width, 0)
        row_cot_block = lax.dynamic_slice_in_dim(all_cot_rows, start, block_width, 0)
        row_scores = logit_scale * dot_rows(text_block, images)
        row_weights = cot_rows[None, :] * jnp.exp(row_scores - row_lse[None, :]) + col_cot_block[
            :, None
        ] * jnp.exp(row_scores - col_lse_block[:, None])
        acc_images = acc_images + dot_lead(row_weights.astype(jnp.bfloat16), text_block)
        col_scores = logit_scale * dot_rows(image_block, texts)
        col_weights = row_cot_block[:, None] * jnp.exp(
            col_scores - row_lse_block[:, None]
        ) + cot_cols[None, :] * jnp.exp(col_scores - col_lse[None, :])
        acc_texts = acc_texts + dot_lead(col_weights.astype(jnp.bfloat16), image_block)
        return (acc_images, acc_texts)

    zero_grads = jnp.zeros((row_count, images.shape[1]), jnp.float32)
    image_terms, text_terms = lax.fori_loop(0, block_count, second_pass, (zero_grads, zero_grads))
    both_cot = (cot_rows + cot_cols)[:, None]
    grad_images = logit_scale * (image_terms - both_cot * texts.astype(jnp.float32))
    grad_texts = logit_scale * (text_terms - both_cot * images.astype(jnp.float32))
    return (row_losses, grad_images, grad_texts)


def solution(mesh):
    return jax.shard_map(
        shards,
        mesh=mesh,
        in_specs=(P(("dp", "blk"), None), P(("dp", "blk"), None), P(), P(None, ("dp", "blk"))),
        out_specs=(P(None, ("dp", "blk")), P(("dp", "blk"), None), P(("dp", "blk"), None)),
        check_vma=False,
    )
```

profile of v0, /device:TPU:0, one launch (start us, length us, event | category | flops | bytes accessed | tf_op | source)
XLA Modules:
  0.0 132.9 jit_solution(15511279975993107705)
XLA Ops:
  7.2 0.0 all-gather.9.cloned.1.call-start
  7.2 0.7 all-gather.9.cloned.1.call-update
  7.9 0.0 all-gather.7.cloned.1.call-start
  7.9 0.7 all-gather.7.cloned.1.call-update
  9.3 0.8 fusion.30
  10.1 22.3 %all-gather = f32[1,1024]{1,0:T(1,128)S(1)} all-gather(f32[1,128]{1,0:T(1,128)S(1)} %get-tuple-element.56), channel_id=2, replica_groups=mesh['blk'=8,'dp'=4] {'blk'}, dimensions={1}, use_global_device_ids=true | all-gather | bytes 4608 | tf_op jit(solution)/shard_map/all_gather | solution.py:70
  32.3 16.5 %all-gather.1 = f32[1,1024]{1,0:T(1,128)S(1)} all-gather(f32[1,128]{1,0:T(1,128)S(1)} %get-tuple-element.53), channel_id=3, replica_groups=mesh['blk'=8,'dp'=4] {'blk'}, dimensions={1}, use_global_device_ids=true | all-gather | bytes 4608 | tf_op jit(solution)/shard_map/all_gather | solution.py:69
  48.9 0.0 copy-start.3
  48.9 1.2 fusion.2
  50.1 0.8 bitcast_add_fusion
  50.8 6.3 %all-gather.9.cloned.1.call-done = bf16[1024,768]{1,0:T(8,128)(2,1)} async-done(((bf16[128,768]{1,0:T(8,128)(2,1)}), bf16[1024,768]{1,0:T(8,128)(2,1)}) %all-gather.9.cloned.1.call-update) | async-done | bytes 1572880 | tf_op jit(solution)/shard_map/all_gather | solution.py:41
  57.1 2.0 %fusion.32 = (f32[128]{0:T(128)S(1)}, f32[1024,128]{1,0:T(8,128)S(1)}) fusion(bf16[1024,768]{1,0:T(8,128)(2,1)} %all-gather.9.cloned.1.call-done, bf16[128,768]{1,0:T(8,128)(2,1)} %param.5, f32[]{:T(128)} %bitcast.83), kind=kOutput, calls=%fused_computation.58 | convolution fusion | flops 201588608 | bytes 2294276 | tf_op jit(solution)/shard_map/while/body/eval_jaxpr/dot_general | solution.py:8
  59.1 0.0 copy-start.2
  59.1 0.2 exponential_reduce_fusion
  59.3 18.1 %all-gather.2 = f32[8,1,128]{2,1,0:T(1,128)S(1)} all-gather(f32[1,1,128]{2,1,0:T(1,128)S(1)} %bitcast.89), channel_id=1, replica_groups=mesh['blk'=8,'dp'=4] {'blk'}, dimensions={0}, use_global_device_ids=true | all-gather | bytes 4608 | tf_op jit(solution)/shard_map/all_gather | solution.py:68
  77.3 24.5 %all-gather.7.cloned.1.call-done = bf16[1024,768]{1,0:T(8,128)(2,1)} async-done(((bf16[128,768]{1,0:T(8,128)(2,1)}), bf16[1024,768]{1,0:T(8,128)(2,1)}) %all-gather.7.cloned.1.call-update) | async-done | bytes 1572880 | tf_op jit(solution)/shard_map/all_gather | solution.py:42
  101.8 0.0 copy-start.1
  101.8 0.0 copy-done.3
  101.8 2.1 %fusion.31 = (f32[128]{0:T(128)S(1)}, f32[1024,128]{1,0:T(8,128)S(1)}) fusion(bf16[1024,768]{1,0:T(8,128)(2,1)} %all-gather.7.cloned.1.call-done, bf16[128,768]{1,0:T(8,128)(2,1)S(1)} %copy-done.3, f32[]{:T(128)} %bitcast.80), kind=kOutput, calls=%fused_computation.57 | convolution fusion | flops 201588608 | bytes 2294276 | tf_op jit(solution)/shard_map/while/body/eval_jaxpr/dot_general | solution.py:8
  103.9 0.0 copy-start
  103.9 0.2 exponential_reduce_fusion.1
  104.1 18.1 %all-gather.3 = f32[8,1,128]{2,1,0:T(1,128)S(1)} all-gather(f32[1,1,128]{2,1,0:T(1,128)S(1)} %bitcast.90), channel_id=1, replica_groups=mesh['blk'=8,'dp'=4] {'blk'}, dimensions={0}, use_global_device_ids=true | all-gather | bytes 4608 | tf_op jit(solution)/shard_map/all_gather | solution.py:67
  122.2 0.6 pad_maximum_fusion
  122.8 0.0 copy-done.2
  122.8 0.0 copy-done.1
  122.8 1.7 %fusion.1 = f32[128,768]{1,0:T(8,128)} fusion(bf16[1024,768]{1,0:T(8,128)(2,1)S(1)} %copy-done.1, bf16[128,768]{1,0:T(8,128)(2,1)S(1)} %copy-done.2, f32[1024,128]{1,0:T(8,128)S(1)} %get-tuple-element.60, f32[1024]{0:T(1024)S(1)} %bitcast.88, f32[1024]{0:T(1024)S(1)} %bitcast.86, f32[128]{0:T(128)S(1)} %log_add_fusion.1, f32[128]{0:T(128)S(1)} %get-tuple-element.54, ...), kind=kOutput, calls=%fused_computation.5 | convolution fusion | flops 202506240 | bytes 2696708 | tf_op jit(solution)/shard_map/while/body/eval_jaxpr/dot_general | solution.py:14
  124.4 0.0 copy-done
  124.4 1.7 %fusion = f32[128,768]{1,0:T(8,128)} fusion(bf16[1024,768]{1,0:T(8,128)(2,1)S(1)} %copy-done, bf16[128,768]{1,0:T(8,128)(2,1)S(1)} %copy-done.3, f32[1024,128]{1,0:T(8,128)S(1)} %get-tuple-element.79, f32[128]{0:T(128)S(1)} %log_add_fusion, f32[128]{0:T(128)S(1)} %get-tuple-element.55, f32[1024]{0:T(1024)S(1)} %bitcast.87, f32[1024]{0:T(1024)S(1)} %bitcast.85, ...), kind=kOutput, calls=%fused_computation.3 | convolution fusion | flops 202506240 | bytes 2696708 | tf_op jit(solution)/shard_map/while/body/eval_jaxpr/dot_general | solution.py:14
  (3 shorter events, 0.0 us)
Async XLA Ops:
  7.2 49.9 %all-gather.9.cloned.1.call-start = ((), (), s32[]{:S(2)}) async-start(), calls=%async_computation.1 | async-start | bytes 1769472 | tf_op jit(solution)/shard_map/all_gather | solution.py:41
  7.9 93.9 %all-gather.7.cloned.1.call-start = ((), (), s32[]{:S(2)}) async-start(), calls=%async_computation | async-start | bytes 1769472 | tf_op jit(solution)/shard_map/all_gather | solution.py:42
  48.9 53.0 %copy-start.3 = (bf16[128,768]{1,0:T(8,128)(2,1)S(1)}, bf16[128,768]{1,0:T(8,128)(2,1)}, u32[]{:S(2)}) copy-start(bf16[128,768]{1,0:T(8,128)(2,1)} %param.4) | copy-start | bytes 589828
  59.1 63.7 %copy-start.2 = (bf16[128,768]{1,0:T(8,128)(2,1)S(1)}, bf16[128,768]{1,0:T(8,128)(2,1)}, u32[]{:S(2)}) copy-start(bf16[128,768]{1,0:T(8,128)(2,1)} %param.5) | copy-start | bytes 589828
  101.8 21.0 %copy-start.1 = (bf16[1024,768]{1,0:T(8,128)(2,1)S(1)}, bf16[1024,768]{1,0:T(8,128)(2,1)}, u32[]{:S(2)}) copy-start(bf16[1024,768]{1,0:T(8,128)(2,1)} %all-gather.7.cloned.1.call-done) | copy-start | bytes 4718596
  103.9 20.5 %copy-start = (bf16[1024,768]{1,0:T(8,128)(2,1)S(1)}, bf16[1024,768]{1,0:T(8,128)(2,1)}, u32[]{:S(2)}) copy-start(bf16[1024,768]{1,0:T(8,128)(2,1)} %all-gather.9.cloned.1.call-done) | copy-start | bytes 4718596
Sparse Core Ops, SparseCore 0:
  10.2 46.9 all-gather.8
  59.3 42.4 all-gather.6
where the time goes:
time: 133 us
  blocking collectives  74.9 us (56%)
  waiting for transfers between devices  32.1 us (24%)
  between operations  14.7 us (11%)
  matrix products  7.41 us (6%)
  other arithmetic  2.9 us (2%)
    all_gather x1, waiting for transfers between devices, shards(): lax.all_gather(texts, 'blk', axis=0, tiled=True)  24.5 us
    all_gather x1, blocking collectives, shards(): lax.all_gather(cot_cols, 'blk', axis=0, tiled=True)  22.3 us
    all_gather x1, blocking collectives, shards(): lax.all_gather(row_lse, 'blk', axis=0, tiled=True)  18.1 us
    all_gather x1, blocking collectives, shards(): lax.all_gather(col_lse, 'blk', axis=0, tiled=True)  18.1 us
    all_gather x1, blocking collectives, shards(): lax.all_gather(cot_rows, 'blk', axis=0, tiled=True)  16.5 us
    all_gather x1, waiting for transfers between devices, shards(): lax.all_gather(images, 'blk', axis=0, tiled=True)  6.28 us
    dot_general x2, matrix products, dot_rows(): lax.dot_general(left, right, (((1,), (1,)), ((), ())), preferred_element_...  4.1 us
    dot_general x2, matrix products, dot_lead(): lax.dot_general(left, right, (((0,), (0,)), ((), ())), preferred_element_...  3.31 us
  transfers between devices with their start and end apart: 2, of which 2 were waited for; matrix products, arithmetic and copies ran while one was open for 4% of the time, Pallas kernels for 0%

commit v1 on v0

--- a/solution.py
+++ b/solution.py
@@ -1,7 +1,255 @@
 import jax
 import jax.numpy as jnp
 from jax import lax
+from jax.experimental import pallas as pl
+from jax.experimental.pallas import tpu as pltpu
 from jax.sharding import PartitionSpec as P
+
+LANES = 128
+MESH = pl.DeviceIdType.MESH
+
+SLOTS = (
+    ((0, 0), (0, 1), (1, 0), (1, 1), (2, 0), (2, 1), (3, 0), (3, 1)),
+    ((1, 0), (1, 1), (0, 0), (2, 0), (0, 1), (3, 0), (2, 1), (3, 1)),
+)
+LINE = len(SLOTS[0]) // 2
+PHASES = (
+    (
+        [
+            ("I", (0, 1), "i"), ("I", (1, 0), "x"), ("T", (0, 1), "i"), ("T", (1, 0), "x"),
+        ],
+        [("I", (1, 1), ""), ("I", (2, 0), "x"), ("T", (1, 1), ""), ("T", (2, 0), "x")],
+        [("I", (2, 1), ""), ("I", (3, 0), "x"), ("T", (2, 1), ""), ("T", (3, 0), "")],
+        [("I", (3, 1), ""), ("T", (3, 1), "")],
+    ),
+    (
+        [
+            ("I", (1, 1), ""), ("I", (0, 0), "i"), ("I", (2, 0), "ox"),
+            ("T", (1, 1), ""), ("T", (0, 0), "i"), ("T", (2, 0), "ox"),
+        ],
+        [
+            ("I", (0, 1), ""), ("I", (3, 0), "o"), ("T", (0, 1), ""),
+            ("T", (3, 0), "ox"), ("I", (3, 0), "X"),
+        ],
+        [("I", (2, 1), ""), ("T", (2, 1), "")],
+        [("T", (3, 1), "o"), ("I", (3, 1), "")],
+    ),
+)
+GROUPS = ((0, 1), (1, 3), (3, 5), (5, 7), (7, 8))
+OWN_WAYS = ("ix", "iox")
+
+
+def landing(half, block, way):
+    place, other = block
+    if way == "x":
+        return half, (place, 1 - other)
+    if way == "o":
+        return half - 1, block
+    if half == LINE // 2 - 1:
+        return half, (LINE - 1 - place, other)
+    return half + 1, block
+
+
+def as_column(row, rows):
+    return jnp.transpose(jnp.broadcast_to(row, (LANES, rows)))
+
+
+def fold(top_ref, sum_ref, tile, low, high, fresh):
+    top = jnp.max(tile, axis=0, keepdims=True)
+    if fresh:
+        sum_ref[:, low:high] = jnp.sum(jnp.exp(tile - top), axis=0, keepdims=True)
+    else:
+        before = top_ref[:, low:high]
+        top = jnp.maximum(before, top)
+        sum_ref[:, low:high] = sum_ref[:, low:high] * jnp.exp(before - top) + jnp.sum(
+            jnp.exp(tile - top), axis=0, keepdims=True
+        )
+    top_ref[:, low:high] = top
+
+
+def kernel(
+    scale_ref, images_ref, texts_ref, cot_ref, losses_ref, grad_images_ref, grad_texts_ref,
+    all_images, all_texts, all_cot, strip_i, strip_t, top_r, sum_r, top_c, sum_c, weights_i, weights_t,
+    send_sem, recv_sem,
+):
+    rows, width = images_ref.shape
+    me = lax.axis_index("blk")
+    place, column = me // 2, lax.rem(me, 2)
+    upper = place // (LINE // 2)
+    step = 1 - 2 * upper
+    from_end = place + upper * (LINE - 1 - 2 * place)
+    peers = {
+        "x": place * 2 + 1 - column,
+        "i": (place + step) * 2 + column,
+        "o": (place - step) * 2 + column,
+    }
+    kinds = "ITC"
+
+    def part(kind, slot):
+        if kind == "C":
+            return all_cot.at[slot]
+        return (all_images if kind == "I" else all_texts).at[pl.ds(slot * rows, rows)]
+
+    def copy(half, kind, block, way):
+        slot = SLOTS[half].index(block)
+        there, name = landing(half, block, way)
+        own = {"I": images_ref, "T": texts_ref, "C": cot_ref}[kind]
+        target = SLOTS[there].index(name)
+        at = kinds.index(kind)
+        return pltpu.make_async_remote_copy(
+            src_ref=own if slot == 0 else part(kind, slot),
+            dst_ref=part(kind, target),
+            send_sem=send_sem.at[at, slot, "xio".index(way)],
+            recv_sem=recv_sem.at[at, target],
+            device_id={"blk": peers[way]},
+            device_id_type=MESH,
+        )
+
+    def arrived(half, kind, block):
+        slot = SLOTS[half].index(block)
+        at = kinds.index(kind)
+        pltpu.make_async_remote_copy(
+            src_ref=part(kind, slot),
+            dst_ref=part(kind, slot),
+            send_sem=send_sem.at[at, slot, 0],
+            recv_sem=recv_sem.at[at, slot],
+            device_id={"blk": peers["x"]},
+            device_id_type=MESH,
+        ).wait_recv()
+
+    def both(kind):
+        return ("C", "T") if kind == "T" else ("I",)
+
+    sent = ([], [])
+
+    def phase(number):
+        for half in range(LINE // 2):
+
+            @pl.when(from_end == half)
+            def _():
+                for kind, block, ways in PHASES[half][number]:
+                    for each in both(kind):
+                        if ways != "X":
+                            arrived(half, each, block)
+                        for way in ways.lower():
+                            one = (half, each, block, way)
+                            copy(*one).start()
+                            sent[half].append(one)
+
+    barrier = pltpu.get_barrier_semaphore()
+    for half in range(LINE // 2):
+
+        @pl.when(from_end == half)
+        def _():
+            for way in OWN_WAYS[half]:
+                pl.semaphore_signal(barrier, inc=1, device_id={"blk": peers[way]}, device_id_type=MESH)
+            pl.semaphore_wait(barrier, len(OWN_WAYS[half]))
+            for kind in "ICT":
+                for way in OWN_WAYS[half]:
+                    one = (half, kind, SLOTS[half][0], way)
+                    copy(*one).start()
+                    sent[half].append(one)
+
+    scale = scale_ref[0]
+    all_images[0:rows, :] = images_ref[...]
+    all_texts[0:rows, :] = texts_ref[...]
+
+    def scores(left, right):
+        return scale * dot_rows(left, right)
+
+    def accumulate(left, right, strip, top, total, low, high):
+        old, new = low * rows, high * rows
+        tile = scores(left[old:new, :], right[0:new, :])
+        fold(top, total, tile[:, old:], old, new, True)
+        if low == 0:
+            strip[:, old:new] = tile
+            return
+        fold(top, total, tile[:, :old], 0, old, False)
+        tile = scores(left[0:old, :], right[old:new, :])
+        strip[:, old:new] = tile[0:rows, :]
+        fold(top, total, tile, old, new, False)
+
+    for number, (low, high) in enumerate(GROUPS):
+        if number:
+            phase(number - 1)
+        accumulate(all_images, all_texts, strip_i, top_c, sum_c, low, high)
+        accumulate(all_texts, all_images, strip_t, top_r, sum_r, low, high)
+
+    row_lse = top_r[...] + jnp.log(sum_r[...])
+    col_lse = top_c[...] + jnp.log(sum_c[...])
+    own_r, own_c = row_lse[:, 0:rows], col_lse[:, 0:rows]
+    cot_r, cot_c = cot_ref[0:1, :], cot_ref[1:2, :]
+    own_r_col, own_c_col = as_column(own_r, rows), as_column(own_c, rows)
+    cot_r_col, cot_c_col = as_column(cot_r, rows), as_column(cot_c, rows)
+    count = all_cot.shape[0]
+    for slot in range(count):
+        r_row = cot_r if slot == 0 else all_cot[slot, 0:1, :]
+        c_row = cot_c if slot == 0 else all_cot[slot, 1:2, :]
+        for at in range(0, rows, LANES):
+            span = slice(slot * rows + at, slot * rows + at + LANES)
+            part_i, part_t = strip_i[:, span], strip_t[:, span]
+            weights_i[:, span] = (
+                cot_r_col * jnp.exp(part_i - own_r_col)
+                + c_row[:, at : at + LANES] * jnp.exp(part_i - col_lse[:, span])
+            ).astype(jnp.bfloat16)
+            weights_t[:, span] = (
+                r_row[:, at : at + LANES] * jnp.exp(part_t - row_lse[:, span])
+                + cot_c_col * jnp.exp(part_t - own_c_col)
+            ).astype(jnp.bfloat16)
+
+    both_cot = cot_r_col + cot_c_col
+    product = jnp.zeros((rows, LANES), jnp.float32)
+    terms_i = jnp.dot(weights_i[...], all_texts[...], preferred_element_type=jnp.float32)
+    terms_t = jnp.dot(weights_t[...], all_images[...], preferred_element_type=jnp.float32)
+    for at in range(0, width, LANES):
+        span = slice(at, at + LANES)
+        image = images_ref[:, span].astype(jnp.float32)
+        text = texts_ref[:, span].astype(jnp.float32)
+        product = product + image * text
+        grad_images_ref[:, span] = scale * (terms_i[:, span] - both_cot * text)
+        grad_texts_ref[:, span] = scale * (terms_t[:, span] - both_cot * image)
+    matched = scale * jnp.sum(jnp.transpose(product), axis=0, keepdims=True)
+    losses_ref[0:1, :] = own_r - matched
+    losses_ref[1:2, :] = own_c - matched
+
+    for half in range(LINE // 2):
+
+        @pl.when(from_end == half)
+        def _():
+            for one in sent[half]:
+                copy(*one).wait_send()
+
+
+def exchange(images, texts, scale, cotangent, count):
+    rows, width = images.shape
+    total = count * rows
+    vmem = pl.BlockSpec(memory_space=pltpu.VMEM)
+    return pl.pallas_call(
+        kernel,
+        out_shape=(
+            jax.ShapeDtypeStruct((2, rows), jnp.float32),
+            jax.ShapeDtypeStruct((rows, width), jnp.float32),
+            jax.ShapeDtypeStruct((rows, width), jnp.float32),
+        ),
+        in_specs=[pl.BlockSpec(memory_space=pltpu.SMEM), vmem, vmem, vmem],
+        out_specs=(vmem, vmem, vmem),
+        scratch_shapes=[
+            pltpu.VMEM((total, width), jnp.bfloat16),
+            pltpu.VMEM((total, width), jnp.bfloat16),
+            pltpu.VMEM((count, 2, rows), jnp.float32),
+            pltpu.VMEM((rows, total), jnp.float32),
+            pltpu.VMEM((rows, total), jnp.float32),
+            pltpu.VMEM((1, total), jnp.float32),
+            pltpu.VMEM((1, total), jnp.float32),
+            pltpu.VMEM((1, total), jnp.float32),
+            pltpu.VMEM((1, total), jnp.float32),
+            pltpu.VMEM((rows, total), jnp.bfloat16),
+            pltpu.VMEM((rows, total), jnp.bfloat16),
+            pltpu.SemaphoreType.DMA((3, count, 3)),
+            pltpu.SemaphoreType.DMA((3, count)),
+        ],
+        compiler_params=pltpu.CompilerParams(collective_id=0, has_side_effects=True),
+    )(scale, images, texts, cotangent)
 
 
 def dot_rows(left, right):
@@ -100,8 +348,15 @@
 
 
 def solution(mesh):
+    count = mesh.shape["blk"]
+
+    def step(images, texts, scale, cotangent):
+        if count == 2 * LINE and images.shape[0] % LANES == 0:
+            return exchange(images, texts, scale, cotangent, count)
+        return shards(images, texts, scale, cotangent)
+
     return jax.shard_map(
-        shards,
+        step,
         mesh=mesh,
         in_specs=(P(("dp", "blk"), None), P(("dp", "blk"), None), P(), P(None, ("dp", "blk"))),
         out_specs=(P(None, ("dp", "blk")), P(("dp", "blk"), None), P(("dp", "blk"), None)),

time: 133 us -> 46.3 us (0.35)
  blocking collectives: 74.9 us -> 0 us
  Pallas kernels: 0 us -> 41 us
  waiting for transfers between devices: 32.1 us -> 0 us
  between operations: 14.7 us -> 1.3 us
  matrix products: 7.41 us -> 0 us
  local copies, waits for them, and re-layouts: 0.78 us -> 3.79 us
  other arithmetic: 2.9 us -> 0 us
    all_gather x4 -> x0, blocking collectives: 74.9 us -> none  [the longest x1 22.3 us: shards(): lax.all_gather(cot_cols, 'blk', axis=0, tiled=True)]
    pallas_call x0 -> x1, Pallas kernels: none -> 41 us  [exchange(): pl.pallas_call(kernel, out_shape=(jax.ShapeDtypeStruct((2, rows), jnp.flo...]
    all_gather x2 -> x0, waiting for transfers between devices: 30.8 us -> none  [the longest x1 24.5 us: shards(): lax.all_gather(texts, 'blk', axis=0, tiled=True)]
    dot_general x4 -> x0, matrix products: 7.41 us -> none  [the longest x2 4.1 us: dot_rows(): lax.dot_general(left, right, (((1,), (1,)), ((), ())), preferred_element_...]
    unnamed x8 -> x7, local copies, waits for them, and re-layouts: 0.02 us -> 3.79 us
    reduce_sum x3 -> x0, other arithmetic: 1.51 us -> none  [the longest x1 1.19 us: shards(): jnp.sum(images.astype(jnp.float32) * texts.astype(jnp.float32), axis=1)]
    unnamed x2 -> x0, waiting for transfers between devices: 1.38 us -> none
  transfers between devices with their start and end apart: 2 -> 0, of which waited for: 2 -> 0; matrix products, arithmetic and copies ran while one was open for 4% -> 0% of each run, Pallas kernels for 0% -> 0%
where the time goes in v1:
time: 46.3 us; the launch traced here: 46.1 us
  Pallas kernels  41 us (89%)
  local copies, waits for them, and re-layouts  3.79 us (8%)
  between operations  1.3 us (3%)
    pallas_call x1, Pallas kernels, exchange(): pl.pallas_call(kernel, out_shape=(jax.ShapeDtypeStruct((2, rows), jnp.flo...  41 us
    unnamed x7, local copies, waits for them, and re-layouts  3.79 us

profile of v1, /device:TPU:0, one launch (start us, length us, event | category | flops | bytes accessed | tf_op | source)
XLA Modules:
  0.0 46.1 jit_solution(9561744037923936622)
XLA Ops:
  1.3 41.0 %shard_map.67 = (f32[2,128]{1,0:T(2,128)}, f32[128,768]{1,0:T(8,128)}, f32[128,768]{1,0:T(8,128)}) custom-call(f32[1]{0:T(128)S(6)} %copy.10.scale_ref, bf16[128,768]{1,0:T(8,128)(2,1)} %images_ref.1, bf16[128,768]{1,0:T(8,128)(2,1)} %texts_ref.1, f32[2,128]{1,0:T(2,128)} %cot_ref.1), custom_call_target="tpu_custom_call" | custom-call | tf_op jit(solution)/shard_map/pallas_call | solution.py:227
  42.3 0.0 copy-start.1
  42.3 0.7 %copy-done.1 = f32[2,128]{1,0:T(2,128)S(1)} copy-done((f32[2,128]{1,0:T(2,128)S(1)}, f32[2,128]{1,0:T(2,128)}, u32[]{:S(2)}) %copy-start.1) | copy-done | bytes 1048
  43.0 0.6 %copy.11 = f32[2,128]{1,0:T(2,128)} copy(f32[2,128]{1,0:T(2,128)S(1)} %copy-done.1) | data formatting | bytes 2048
  43.5 0.0 copy-start
  43.5 1.8 %copy.12 = f32[128,768]{1,0:T(8,128)} copy(f32[128,768]{1,0:T(8,128)} %get-tuple-element.7) | data formatting | bytes 786432
  45.4 0.0 copy-done
  45.4 0.7 %copy.13 = f32[128,768]{1,0:T(8,128)} copy(f32[128,768]{1,0:T(8,128)S(1)} %copy-done) | data formatting | bytes 786432
Async XLA Ops:
  42.3 0.7 %copy-start.1 = (f32[2,128]{1,0:T(2,128)S(1)}, f32[2,128]{1,0:T(2,128)}, u32[]{:S(2)}) copy-start(f32[2,128]{1,0:T(2,128)} %get-tuple-element.6) | copy-start | bytes 3076
  43.5 1.8 %copy-start = (f32[128,768]{1,0:T(8,128)S(1)}, f32[128,768]{1,0:T(8,128)}, u32[]{:S(2)}) copy-start(f32[128,768]{1,0:T(8,128)} %get-tuple-element.8) | copy-start | bytes 1179652

commit v2 on v1

--- a/solution.py
+++ b/solution.py
@@ -6,6 +6,8 @@
 from jax.sharding import PartitionSpec as P
 
 LANES = 128
+VMEM_BYTES = 67043328
+MARGIN = 4096
 MESH = pl.DeviceIdType.MESH
 
 SLOTS = (
@@ -68,9 +70,9 @@
 
 
 def kernel(
-    scale_ref, images_ref, texts_ref, cot_ref, losses_ref, grad_images_ref, grad_texts_ref,
-    all_images, all_texts, all_cot, strip_i, strip_t, top_r, sum_r, top_c, sum_c, weights_i, weights_t,
-    send_sem, recv_sem,
+    scale_ref, images_ref, texts_ref, cot_ref,
+    all_images, all_texts, all_cot, weights_i, weights_t, lses_ref,
+    strip_i, strip_t, top_r, sum_r, top_c, sum_c, send_sem, recv_sem, own_sem,
 ):
     rows, width = images_ref.shape
     me = lax.axis_index("blk")
@@ -136,6 +138,10 @@
                             copy(*one).start()
                             sent[half].append(one)
 
+    mine = [
+        pltpu.make_async_copy(source, part(kind, 0), own_sem.at[kinds.index(kind)])
+        for kind, source in zip(kinds, (images_ref, texts_ref, cot_ref))
+    ]
     barrier = pltpu.get_barrier_semaphore()
     for half in range(LINE // 2):
 
@@ -151,8 +157,10 @@
                     sent[half].append(one)
 
     scale = scale_ref[0]
-    all_images[0:rows, :] = images_ref[...]
-    all_texts[0:rows, :] = texts_ref[...]
+    for each in mine:
+        each.start()
+    for each in mine:
+        each.wait()
 
     def scores(left, right):
         return scale * dot_rows(left, right)
@@ -178,13 +186,14 @@
     row_lse = top_r[...] + jnp.log(sum_r[...])
     col_lse = top_c[...] + jnp.log(sum_c[...])
     own_r, own_c = row_lse[:, 0:rows], col_lse[:, 0:rows]
-    cot_r, cot_c = cot_ref[0:1, :], cot_ref[1:2, :]
+    lses_ref[0:1, :] = own_r
+    lses_ref[1:2, :] = own_c
+    cot_r, cot_c = all_cot[0, 0:1, :], all_cot[0, 1:2, :]
     own_r_col, own_c_col = as_column(own_r, rows), as_column(own_c, rows)
     cot_r_col, cot_c_col = as_column(cot_r, rows), as_column(cot_c, rows)
     count = all_cot.shape[0]
     for slot in range(count):
-        r_row = cot_r if slot == 0 else all_cot[slot, 0:1, :]
-        c_row = cot_c if slot == 0 else all_cot[slot, 1:2, :]
+        r_row, c_row = all_cot[slot, 0:1, :], all_cot[slot, 1:2, :]
         for at in range(0, rows, LANES):
             span = slice(slot * rows + at, slot * rows + at + LANES)
             part_i, part_t = strip_i[:, span], strip_t[:, span]
@@ -197,21 +206,6 @@
                 + cot_c_col * jnp.exp(part_t - own_c_col)
             ).astype(jnp.bfloat16)
 
-    both_cot = cot_r_col + cot_c_col
-    product = jnp.zeros((rows, LANES), jnp.float32)
-    terms_i = jnp.dot(weights_i[...], all_texts[...], preferred_element_type=jnp.float32)
-    terms_t = jnp.dot(weights_t[...], all_images[...], preferred_element_type=jnp.float32)
-    for at in range(0, width, LANES):
-        span = slice(at, at + LANES)
-        image = images_ref[:, span].astype(jnp.float32)
-        text = texts_ref[:, span].astype(jnp.float32)
-        product = product + image * text
-        grad_images_ref[:, span] = scale * (terms_i[:, span] - both_cot * text)
-        grad_texts_ref[:, span] = scale * (terms_t[:, span] - both_cot * image)
-    matched = scale * jnp.sum(jnp.transpose(product), axis=0, keepdims=True)
-    losses_ref[0:1, :] = own_r - matched
-    losses_ref[1:2, :] = own_c - matched
-
     for half in range(LINE // 2):
 
         @pl.when(from_end == half)
@@ -220,36 +214,90 @@
                 copy(*one).wait_send()
 
 
+def finish(
+    scale_ref, all_images, all_texts, all_cot, weights_i, weights_t, lses_ref,
+    losses_ref, grad_images_ref, grad_texts_ref, losses, grad_images, grad_texts, sem,
+):
+    rows, width = grad_images.shape
+    scale = scale_ref[0]
+    both_cot = as_column(all_cot[0, 0:1, :] + all_cot[0, 1:2, :], rows)
+    outs = [
+        pltpu.make_async_copy(*pair, sem.at[at])
+        for at, pair in enumerate(
+            ((grad_images, grad_images_ref), (grad_texts, grad_texts_ref), (losses, losses_ref))
+        )
+    ]
+    terms = jnp.dot(weights_i[...], all_texts[...], preferred_element_type=jnp.float32)
+    product = jnp.zeros((rows, LANES), jnp.float32)
+    for at in range(0, width, LANES):
+        span = slice(at, at + LANES)
+        text = all_texts[0:rows, span].astype(jnp.float32)
+        product = product + all_images[0:rows, span].astype(jnp.float32) * text
+        grad_images[:, span] = scale * (terms[:, span] - both_cot * text)
+    outs[0].start()
+    matched = scale * jnp.sum(jnp.transpose(product), axis=0, keepdims=True)
+    losses[...] = lses_ref[...] - matched
+    outs[2].start()
+    terms = jnp.dot(weights_t[...], all_images[...], preferred_element_type=jnp.float32)
+    for at in range(0, width, LANES):
+        span = slice(at, at + LANES)
+        image = all_images[0:rows, span].astype(jnp.float32)
+        grad_texts[:, span] = scale * (terms[:, span] - both_cot * image)
+    outs[1].start()
+    for out in outs:
+        out.wait()
+
+
 def exchange(images, texts, scale, cotangent, count):
     rows, width = images.shape
     total = count * rows
     vmem = pl.BlockSpec(memory_space=pltpu.VMEM)
-    return pl.pallas_call(
+    smem = pl.BlockSpec(memory_space=pltpu.SMEM)
+    hbm = pl.BlockSpec(memory_space=pltpu.HBM)
+    f32, bf16 = jnp.float32, jnp.bfloat16
+    kept = (
+        pltpu.VMEM((total, width), bf16),
+        pltpu.VMEM((total, width), bf16),
+        pltpu.VMEM((count, 2, rows), f32),
+        pltpu.VMEM((rows, total), bf16),
+        pltpu.VMEM((rows, total), bf16),
+        pltpu.VMEM((2, rows), f32),
+    )
+    handed_on = 2 * total * (2 * width + 2 * rows) + 4 * 2 * rows * (count + 1)
+    grant = VMEM_BYTES - handed_on - MARGIN
+    gathered = pl.pallas_call(
         kernel,
-        out_shape=(
-            jax.ShapeDtypeStruct((2, rows), jnp.float32),
-            jax.ShapeDtypeStruct((rows, width), jnp.float32),
-            jax.ShapeDtypeStruct((rows, width), jnp.float32),
-        ),
-        in_specs=[pl.BlockSpec(memory_space=pltpu.SMEM), vmem, vmem, vmem],
-        out_specs=(vmem, vmem, vmem),
+        out_shape=kept,
+        in_specs=[smem, hbm, hbm, hbm],
+        out_specs=(vmem,) * len(kept),
         scratch_shapes=[
-            pltpu.VMEM((total, width), jnp.bfloat16),
-            pltpu.VMEM((total, width), jnp.bfloat16),
-            pltpu.VMEM((count, 2, rows), jnp.float32),
-            pltpu.VMEM((rows, total), jnp.float32),
-            pltpu.VMEM((rows, total), jnp.float32),
-            pltpu.VMEM((1, total), jnp.float32),
-            pltpu.VMEM((1, total), jnp.float32),
-            pltpu.VMEM((1, total), jnp.float32),
-            pltpu.VMEM((1, total), jnp.float32),
-            pltpu.VMEM((rows, total), jnp.bfloat16),
-            pltpu.VMEM((rows, total), jnp.bfloat16),
+            pltpu.VMEM((rows, total), f32),
+            pltpu.VMEM((rows, total), f32),
+            pltpu.VMEM((1, total), f32),
+            pltpu.VMEM((1, total), f32),
+            pltpu.VMEM((1, total), f32),
+            pltpu.VMEM((1, total), f32),
             pltpu.SemaphoreType.DMA((3, count, 3)),
             pltpu.SemaphoreType.DMA((3, count)),
+            pltpu.SemaphoreType.DMA((3,)),
         ],
-        compiler_params=pltpu.CompilerParams(collective_id=0, has_side_effects=True),
+        compiler_params=pltpu.CompilerParams(
+            collective_id=0, has_side_effects=True, vmem_limit_bytes=grant
+        ),
     )(scale, images, texts, cotangent)
+    outs = (
+        jax.ShapeDtypeStruct((2, rows), f32),
+        jax.ShapeDtypeStruct((rows, width), f32),
+        jax.ShapeDtypeStruct((rows, width), f32),
+    )
+    return pl.pallas_call(
+        finish,
+        out_shape=outs,
+        in_specs=[smem] + [vmem] * len(kept),
+        out_specs=(hbm,) * len(outs),
+        scratch_shapes=[pltpu.VMEM(out.shape, f32) for out in outs] + [pltpu.SemaphoreType.DMA((3,))],
+        compiler_params=pltpu.CompilerParams(vmem_limit_bytes=grant // 2),
+    )(scale, *gathered)
 
 
 def dot_rows(left, right):

time: 46.3 us -> 41.2 us (0.89)
  local copies, waits for them, and re-layouts: 3.79 us -> 0 us
  Pallas kernels: 41 us -> 39.8 us
    unnamed x7 -> x0, local copies, waits for them, and re-layouts: 3.79 us -> none
    pallas_call x1 -> x2, Pallas kernels: 41 us -> 39.8 us  [the longest x1 38.3 us: exchange(): pl.pallas_call(kernel, out_shape=kept, in_specs=[smem, hbm, hbm, hbm], ou...]
where the time goes in v2:
time: 41.2 us; the launch traced here: 41 us
  Pallas kernels  39.8 us (97%)
  between operations  1.29 us (3%)
    pallas_call x1, Pallas kernels, exchange(): pl.pallas_call(kernel, out_shape=kept, in_specs=[smem, hbm, hbm, hbm], ou...  38.3 us
    pallas_call x1, Pallas kernels, exchange(): pl.pallas_call(finish, out_shape=outs, in_specs=[smem] + [vmem] * len(kep...  1.42 us

profile of v2, /device:TPU:0, one launch (start us, length us, event | category | flops | bytes accessed | tf_op | source)
XLA Modules:
  0.0 41.0 jit_solution(6324070828526376945)
XLA Ops:
  1.3 38.3 %shard_map.67 = (bf16[1024,768]{1,0:T(8,128)(2,1)S(1)}, bf16[1024,768]{1,0:T(8,128)(2,1)S(1)}, f32[8,2,128]{2,1,0:T(2,128)S(1)}, bf16[128,1024]{1,0:T(8,128)(2,1...) custom-call(f32[1]{0:T(128)S(6)} %copy.7.scale_ref, bf16[128,768]{1,0:T(8,128)(2,1)} %images_ref.1, ...), custom_call_target="tpu_custom_call" | custom-call | tf_op jit(solution)/shard_map/pallas_call | solution.py:268
  39.6 1.4 %shard_map.68 = (f32[2,128]{1,0:T(2,128)}, f32[128,768]{1,0:T(8,128)}, f32[128,768]{1,0:T(8,128)}) custom-call(f32[1]{0:T(128)S(6)} %copy.7.scale_ref, bf16[1024,768]{1,0:T(8,128)(2,1)S(1)} %get-tuple-element.9.all_images, bf16[1024,768]{1,0:T(8,128)(2,1)S(1)} %get-tuple-element.10.all_texts, f32[8,2,128]{2,1,0:T(2,128)S(1)} %get-tuple-element.11.all_cot, ...), custom_call_target="tpu_custom_call" | custom-call | tf_op jit(solution)/shard_map/pallas_call | solution.py:293

commit v3 on v2

--- a/solution.py
+++ b/solution.py
@@ -33,8 +33,8 @@
             ("I", (0, 1), ""), ("I", (3, 0), "o"), ("T", (0, 1), ""),
             ("T", (3, 0), "ox"), ("I", (3, 0), "X"),
         ],
-        [("I", (2, 1), ""), ("T", (2, 1), "")],
-        [("T", (3, 1), "o"), ("I", (3, 1), "")],
+        [("I", (2, 1), ""), ("T", (2, 1), ""), ("T", (3, 1), "o")],
+        [("I", (3, 1), "")],
     ),
 )
 GROUPS = ((0, 1), (1, 3), (3, 5), (5, 7), (7, 8))

time: 41.2 us -> 41.2 us (level)
  no operation moved by 1% of the time
where the time goes in v3:
time: 41.2 us; the launch traced here: 41 us
  Pallas kernels  39.8 us (97%)
  between operations  1.29 us (3%)
    pallas_call x1, Pallas kernels, exchange(): pl.pallas_call(kernel, out_shape=kept, in_specs=[smem, hbm, hbm, hbm], ou...  38.3 us
    pallas_call x1, Pallas kernels, exchange(): pl.pallas_call(finish, out_shape=outs, in_specs=[smem] + [vmem] * len(kep...  1.42 us

profile of v3, /device:TPU:0, one launch (start us, length us, event | category | flops | bytes accessed | tf_op | source)
XLA Modules:
  0.0 41.0 jit_solution(7250935000075645427)
XLA Ops:
  1.3 38.3 %shard_map.67 = (bf16[1024,768]{1,0:T(8,128)(2,1)S(1)}, bf16[1024,768]{1,0:T(8,128)(2,1)S(1)}, f32[8,2,128]{2,1,0:T(2,128)S(1)}, bf16[128,1024]{1,0:T(8,128)(2,1...) custom-call(f32[1]{0:T(128)S(6)} %copy.7.scale_ref, bf16[128,768]{1,0:T(8,128)(2,1)} %images_ref.1, ...), custom_call_target="tpu_custom_call" | custom-call | tf_op jit(solution)/shard_map/pallas_call | solution.py:268
  39.6 1.4 %shard_map.68 = (f32[2,128]{1,0:T(2,128)}, f32[128,768]{1,0:T(8,128)}, f32[128,768]{1,0:T(8,128)}) custom-call(f32[1]{0:T(128)S(6)} %copy.7.scale_ref, bf16[1024,768]{1,0:T(8,128)(2,1)S(1)} %get-tuple-element.9.all_images, bf16[1024,768]{1,0:T(8,128)(2,1)S(1)} %get-tuple-element.10.all_texts, f32[8,2,128]{2,1,0:T(2,128)S(1)} %get-tuple-element.11.all_cot, ...), custom_call_target="tpu_custom_call" | custom-call | tf_op jit(solution)/shard_map/pallas_call | solution.py:293

commit v4 on v2

--- a/solution.py
+++ b/solution.py
@@ -72,7 +72,7 @@
 def kernel(
     scale_ref, images_ref, texts_ref, cot_ref,
     all_images, all_texts, all_cot, weights_i, weights_t, lses_ref,
-    strip_i, strip_t, top_r, sum_r, top_c, sum_c, send_sem, recv_sem, own_sem,
+    strip_i, strip_t, top_r, sum_r, top_c, sum_c, scale_own, send_sem, recv_sem, own_sem,
 ):
     rows, width = images_ref.shape
     me = lax.axis_index("blk")
@@ -141,7 +141,7 @@
     mine = [
         pltpu.make_async_copy(source, part(kind, 0), own_sem.at[kinds.index(kind)])
         for kind, source in zip(kinds, (images_ref, texts_ref, cot_ref))
-    ]
+    ] + [pltpu.make_async_copy(scale_ref, scale_own, own_sem.at[len(kinds)])]
     barrier = pltpu.get_barrier_semaphore()
     for half in range(LINE // 2):
 
@@ -156,11 +156,12 @@
                     copy(*one).start()
                     sent[half].append(one)
 
-    scale = scale_ref[0]
     for each in mine:
         each.start()
     for each in mine:
         each.wait()
+
+    scale = scale_own[...]
 
     def scores(left, right):
         return scale * dot_rows(left, right)
@@ -188,6 +189,7 @@
     own_r, own_c = row_lse[:, 0:rows], col_lse[:, 0:rows]
     lses_ref[0:1, :] = own_r
     lses_ref[1:2, :] = own_c
+    lses_ref[2:3, :] = jnp.broadcast_to(scale, (1, rows))
     cot_r, cot_c = all_cot[0, 0:1, :], all_cot[0, 1:2, :]
     own_r_col, own_c_col = as_column(own_r, rows), as_column(own_c, rows)
     cot_r_col, cot_c_col = as_column(cot_r, rows), as_column(cot_c, rows)
@@ -215,11 +217,11 @@
 
 
 def finish(
-    scale_ref, all_images, all_texts, all_cot, weights_i, weights_t, lses_ref,
+    all_images, all_texts, all_cot, weights_i, weights_t, lses_ref,
     losses_ref, grad_images_ref, grad_texts_ref, losses, grad_images, grad_texts, sem,
 ):
     rows, width = grad_images.shape
-    scale = scale_ref[0]
+    scale = lses_ref[2:3, 0:LANES]
     both_cot = as_column(all_cot[0, 0:1, :] + all_cot[0, 1:2, :], rows)
     outs = [
         pltpu.make_async_copy(*pair, sem.at[at])
@@ -235,8 +237,8 @@
         product = product + all_images[0:rows, span].astype(jnp.float32) * text
         grad_images[:, span] = scale * (terms[:, span] - both_cot * text)
     outs[0].start()
-    matched = scale * jnp.sum(jnp.transpose(product), axis=0, keepdims=True)
-    losses[...] = lses_ref[...] - matched
+    matched = lses_ref[2:3, :] * jnp.sum(jnp.transpose(product), axis=0, keepdims=True)
+    losses[...] = lses_ref[0:2, :] - matched
     outs[2].start()
     terms = jnp.dot(weights_t[...], all_images[...], preferred_element_type=jnp.float32)
     for at in range(0, width, LANES):
@@ -252,7 +254,6 @@
     rows, width = images.shape
     total = count * rows
     vmem = pl.BlockSpec(memory_space=pltpu.VMEM)
-    smem = pl.BlockSpec(memory_space=pltpu.SMEM)
     hbm = pl.BlockSpec(memory_space=pltpu.HBM)
     f32, bf16 = jnp.float32, jnp.bfloat16
     kept = (
@@ -261,14 +262,14 @@
         pltpu.VMEM((count, 2, rows), f32),
         pltpu.VMEM((rows, total), bf16),
         pltpu.VMEM((rows, total), bf16),
-        pltpu.VMEM((2, rows), f32),
-    )
-    handed_on = 2 * total * (2 * width + 2 * rows) + 4 * 2 * rows * (count + 1)
+        pltpu.VMEM((3, rows), f32),
+    )
+    handed_on = 2 * total * (2 * width + 2 * rows) + 4 * 2 * rows * (count + 2)
     grant = VMEM_BYTES - handed_on - MARGIN
     gathered = pl.pallas_call(
         kernel,
         out_shape=kept,
-        in_specs=[smem, hbm, hbm, hbm],
+        in_specs=[hbm, hbm, hbm, hbm],
         out_specs=(vmem,) * len(kept),
         scratch_shapes=[
             pltpu.VMEM((rows, total), f32),
@@ -277,14 +278,15 @@
             pltpu.VMEM((1, total), f32),
             pltpu.VMEM((1, total), f32),
             pltpu.VMEM((1, total), f32),
+            pltpu.VMEM((1, 1), f32),
             pltpu.SemaphoreType.DMA((3, count, 3)),
             pltpu.SemaphoreType.DMA((3, count)),
-            pltpu.SemaphoreType.DMA((3,)),
+            pltpu.SemaphoreType.DMA((4,)),
         ],
         compiler_params=pltpu.CompilerParams(
             collective_id=0, has_side_effects=True, vmem_limit_bytes=grant
         ),
-    )(scale, images, texts, cotangent)
+    )(scale.reshape(1, 1), images, texts, cotangent)
     outs = (
         jax.ShapeDtypeStruct((2, rows), f32),
         jax.ShapeDtypeStruct((rows, width), f32),
@@ -293,11 +295,11 @@
     return pl.pallas_call(
         finish,
         out_shape=outs,
-        in_specs=[smem] + [vmem] * len(kept),
+        in_specs=[vmem] * len(kept),
         out_specs=(hbm,) * len(outs),
         scratch_shapes=[pltpu.VMEM(out.shape, f32) for out in outs] + [pltpu.SemaphoreType.DMA((3,))],
         compiler_params=pltpu.CompilerParams(vmem_limit_bytes=grant // 2),
-    )(scale, *gathered)
+    )(*gathered)
 
 
 def dot_rows(left, right):

time: 41.2 us -> 41.2 us (level)
  no operation moved by 1% of the time
where the time goes in v4:
time: 41.2 us; the launch traced here: 41.1 us
  Pallas kernels  39.8 us (97%)
  between operations  1.28 us (3%)
    pallas_call x1, Pallas kernels, exchange(): pl.pallas_call(kernel, out_shape=kept, in_specs=[hbm, hbm, hbm, hbm], out...  38.4 us
    pallas_call x1, Pallas kernels, exchange(): pl.pallas_call(finish, out_shape=outs, in_specs=[vmem] * len(kept), out_s...  1.42 us

profile of v4, /device:TPU:0, one launch (start us, length us, event | category | flops | bytes accessed | tf_op | source)
XLA Modules:
  0.0 41.1 jit_solution(8773903914662315075)
XLA Ops:
  1.3 38.4 %shard_map.67 = (bf16[1024,768]{1,0:T(8,128)(2,1)S(1)}, bf16[1024,768]{1,0:T(8,128)(2,1)S(1)}, f32[8,2,128]{2,1,0:T(2,128)S(1)}, bf16[128,1024]{1,0:T(8,128)(2,1...) custom-call(f32[1,1]{1,0:T(1,128)} %bitcast.1.scale_ref, bf16[128,768]{1,0:T(8,128)(2,1)} %images_ref.1, ...), custom_call_target="tpu_custom_call" | custom-call | tf_op jit(solution)/shard_map/pallas_call | solution.py:269
  39.7 1.4 %shard_map.68 = (f32[2,128]{1,0:T(2,128)}, f32[128,768]{1,0:T(8,128)}, f32[128,768]{1,0:T(8,128)}) custom-call(bf16[1024,768]{1,0:T(8,128)(2,1)S(1)} %get-tuple-element.9.all_images, bf16[1024,768]{1,0:T(8,128)(2,1)S(1)} %get-tuple-element.10.all_texts, f32[8,2,128]{2,1,0:T(2,128)S(1)} %get-tuple-element.11.all_cot, ...), custom_call_target="tpu_custom_call" | custom-call | tf_op jit(solution)/shard_map/pallas_call | solution.py:295
